TPU v7x, 32 devices: a whole 2x2x4 slice. The times are simulated.
32 devices in a mesh: lon: 4 (over z), lat: 8 (over y, x, core).
Axes of the slice: x: 2, y: 2, z: 4, core: 2. Of those that a mesh axis runs over, the one named last changes fastest.
Arguments:
- travel_times: float32 [1024], P(('lon', 'lat')), may hold values from -6 to 6
- ray_counts: int32 [32], P(('lon', 'lat')), may hold values from 4 to 32
- tile_brick: int32 [1024, 4], P(('lon', 'lat')), may hold values from 0 to 31, all different within a row; in each aligned block of 32 rows (0 to 31, 32 to 63, ...) at most 8 rows name the same one
- cell_offsets: int32 [1024, 4, 128], P(('lon', 'lat')), may hold values from 0 to 1023
- cell_depths: int32 [1024, 4, 128], P(('lon', 'lat')), may hold values from 0 to 127
- seg_lengths: float32 [1024, 4, 128], P(('lon', 'lat')), may hold values from 0.002 to 0.02
Outputs:
- model: float32 [128, 256, 128], P('lon', 'lat')
- misfit: float32 [1024], P(('lon', 'lat'))
Inputs may be any that keep to these rules, and one draw needn't show every extreme that they name: `tile_brick`: among the 4 tiles of all rays of one device, no brick is named more than 8 times, a bound that some block reaches; a ray's tiles name different bricks; brick k lives on the device at position k of lon+lat. Only the first ray_counts rays of a device's 32 slots are live.
All inputs are finite; a program needn't handle non-finite values.
Results may differ from a plain program's by a relative error of at most 0.0014.
Values sent between devices are 32-bit elements; how exact they have to be, the bound alone decides.
No kernel may reach another device: no remote copies, remote signals or barrier semaphores. Data moves between devices by JAX's collectives and lax.ppermute only.
A program may use at most 64 MiB of HBM per device.

v0:
```python
import jax
import jax.numpy as jnp
from jax import lax
from jax.sharding import PartitionSpec as P

CLON = 32
CLAT = 32
DEP = 128
ITERS = 2


damping = 0.01


def padded(array, sides, width, wrap):
    for axis, dim in sides:
        devices, length = (lax.axis_size(axis), array.shape[dim])
        up = [(i, (i + 1) % devices) for i in range(devices if wrap else devices - 1)]
        down = [(j, i) for i, j in up]
        last = lax.slice_in_dim(array, length - width, length, axis=dim)
        leading = lax.slice_in_dim(array, 0, width, axis=dim)
        before = lax.ppermute(last, axis, up)
        after = lax.ppermute(leading, axis, down)
        array = jnp.concatenate([before, array, after], axis=dim)
    return array


def shards(travel_times, ray_counts, tile_brick, cell_offsets, cell_depths, seg_lengths):
    devices = lax.axis_size(("lon", "lat"))
    rays_dev, per_ray, seg_count = cell_offsets.shape
    tiles = rays_dev * per_ray
    slots = 2 * tiles
    capacity = slots // devices
    brick_cells = CLON * CLAT * DEP
    inside = cell_offsets * DEP + cell_depths
    live_mask = (jnp.arange(rays_dev, dtype=jnp.int32) < ray_counts[0]).astype(jnp.float32)
    weights = seg_lengths * live_mask[:, None, None]
    bricks = tile_brick.reshape(tiles)
    onehot = (bricks[:, None] == jnp.arange(devices, dtype=jnp.int32)[None, :]).astype(jnp.int32)
    earlier = jnp.cumsum(onehot, axis=0) - onehot
    rank_in = jnp.sum(earlier * onehot, axis=1)
    slot_index = bricks * capacity + rank_in
    send_offs = (
        jnp.zeros((slots, seg_count), jnp.int32)
        .at[slot_index]
        .set(inside.reshape(tiles, seg_count))
    )
    send_lens = (
        jnp.zeros((slots, seg_count), jnp.float32)
        .at[slot_index]
        .set(weights.reshape(tiles, seg_count))
    )
    held_offs, held_lens = (
        lax.all_to_all(send_offs, ("lon", "lat"), split_axis=0, concat_axis=0, tiled=True),
        lax.all_to_all(send_lens, ("lon", "lat"), split_axis=0, concat_axis=0, tiled=True),
    )

    def forward(grid):
        cells = grid.reshape(brick_cells)
        partial_value = jnp.sum(held_lens * cells[held_offs], axis=1)
        returned = lax.all_to_all(
            partial_value, ("lon", "lat"), split_axis=0, concat_axis=0, tiled=True
        )
        return jnp.sum(returned[slot_index].reshape(rays_dev, per_ray), axis=1)

    def backward(ray_vals):
        per_tile = jnp.broadcast_to(ray_vals[:, None], (rays_dev, per_ray)).reshape(tiles)
        slot_vals = jnp.zeros((slots,), jnp.float32).at[slot_index].set(per_tile)
        arrived = lax.all_to_all(slot_vals, ("lon", "lat"), split_axis=0, concat_axis=0, tiled=True)
        terms = held_lens * arrived[:, None]
        cells = (
            jnp.zeros((brick_cells,), jnp.float32).at[held_offs.reshape(-1)].add(terms.reshape(-1))
        )
        return cells.reshape(CLON, CLAT, DEP)

    def smoothing(field):
        lon_pad = padded(field, (("lon", 0),), 1, True)
        lat_pad = padded(field, (("lat", 1),), 1, False)
        dep_pad = jnp.pad(field, ((0, 0), (0, 0), (1, 1)))
        result = 6.0 * field - lon_pad[2:] - lon_pad[:-2] - lat_pad[:, 2:] - lat_pad[:, :-2]
        return result - dep_pad[:, :, 2:] - dep_pad[:, :, :-2]

    def beta_total(ray_part, grid_part):
        return lax.psum(
            jnp.sum(ray_part * ray_part) + jnp.sum(grid_part * grid_part), ("lon", "lat")
        )

    def alpha_total(grid_part):
        return lax.psum(jnp.sum(grid_part * grid_part), ("lon", "lat"))

    data = travel_times * live_mask
    u_grid = jnp.zeros((CLON, CLAT, DEP), jnp.float32)
    beta_now = jnp.sqrt(beta_total(data, u_grid))
    u_ray = data / beta_now
    v_dir = backward(u_ray)
    alpha_now = jnp.sqrt(alpha_total(v_dir))
    v_dir = v_dir / alpha_now
    search = v_dir
    model = jnp.zeros_like(v_dir)
    phi_bar = beta_now
    rho_bar = alpha_now
    for turn_index in range(ITERS):
        p_ray = forward(v_dir) - alpha_now * u_ray
        p_grid = damping * smoothing(v_dir) - alpha_now * u_grid
        beta_now = jnp.sqrt(beta_total(p_ray, p_grid))
        u_ray = p_ray / beta_now
        u_grid = p_grid / beta_now
        v_dir = backward(u_ray) + damping * smoothing(u_grid) - beta_now * v_dir
        alpha_now = jnp.sqrt(alpha_total(v_dir))
        v_dir = v_dir / alpha_now
        rho_new = jnp.sqrt(rho_bar * rho_bar + beta_now * beta_now)
        cosine = rho_bar / rho_new
        sine_val = beta_now / rho_new
        theta_val = sine_val * alpha_now
        rho_bar = -cosine * alpha_now
        phi_val = cosine * phi_bar
        phi_bar = sine_val * phi_bar
        model = model + phi_val / rho_new * search
        search = v_dir - theta_val / rho_new * search
    misfit = data - forward(model)
    return (model, misfit)


def solution(mesh):
    placed = (
        P(("lon", "lat")),
        P(("lon", "lat")),
        P(("lon", "lat"), None),
        P(("lon", "lat"), None, None),
        P(("lon", "lat"), None, None),
        P(("lon", "lat"), None, None),
    )
    return jax.shard_map(
        shards,
        mesh=mesh,
        in_specs=placed,
        out_specs=(P("lon", "lat", None), P(("lon", "lat"))),
        check_vma=False,
    )
```

profile of v0, /device:TPU:0, one launch (start us, length us, event | category | flops | bytes accessed | tf_op | source)
XLA Modules:
  0.0 1280.2 jit_solution(7676610893865908481)
XLA Ops:
  2.7 42.2 %psum.35 = f32[]{:T(128)} all-reduce(f32[]{:T(128)} %multiply_reduce_fusion.5), channel_id=1, replica_groups=mesh['lon'=4,'lat'=8] {'lon','lat'}, use_global_device_ids=true, to_apply=%region_5.6 | all-reduce | flops 1 | bytes 8 | tf_op jit(solution)/shard_map/psum | solution.py:84
  48.2 4.6 all-to-all-start.2
  52.9 1.5 scatter_custom_fusion
  54.4 5.6 all-to-all-done.2
  60.0 2.7 all-to-all-start
  62.9 1.5 scatter_custom_fusion.1
  65.6 5.3 all-to-all-done
  70.9 2.6 all-to-all-start.1
  73.7 8.1 all-to-all-done.1
  81.8 204.6 %scatter_custom_fusion.3 = f32[131072]{0:T(1024)S(1)} fusion(s32[32768]{0:T(1024)S(1)} %bitcast.76, f32[32768]{0:T(1024)S(1)} %bitcast_multiply_fusion.4, f32[]{:T(128)} %constant.8.clone.1), kind=kCustom, calls=%fused_computation.68 | custom fusion | flops 32768 | bytes 524292 | tf_op jit(solution)/shard_map/scatter-add | solution.py:72
  287.2 44.0 %psum.36 = f32[]{:T(128)} all-reduce(f32[]{:T(128)} %multiply_reduce_fusion.2), channel_id=1, replica_groups=mesh['lon'=4,'lat'=8] {'lon','lat'}, use_global_device_ids=true, to_apply=%region_9.10 | all-reduce | flops 1 | bytes 8 | tf_op jit(solution)/shard_map/psum | solution.py:89
  332.0 180.5 %gather_fusion = f32[32768]{0:T(1024)S(1)} fusion(f32[131072]{0:T(1024)S(1)} %broadcast_divide_fusion.2, s32[32768]{0:T(1024)S(1)} %fusion.32), kind=kCustom, calls=%fused_computation | custom fusion | bytes 393216 | tf_op jit(solution)/shard_map/gather | solution.py:60
  513.3 5.2 all-to-all-start.3
  518.5 1.3 collective-permute-start.2
  519.8 3.0 collective-permute-start.3
  522.8 3.7 collective-permute-start
  529.4 2.7 collective-permute-done.1
  534.5 37.7 %psum.37 = f32[]{:T(128)} all-reduce(f32[]{:T(128)S(6)} %add.97), channel_id=1, replica_groups=mesh['lon'=4,'lat'=8] {'lon','lat'}, use_global_device_ids=true, to_apply=%region_14.15 | all-reduce | flops 1 | bytes 8 | tf_op jit(solution)/shard_map/psum | solution.py:84
  574.9 5.9 all-to-all-start.4
  581.0 3.7 collective-permute-start.4
  585.9 3.0 collective-permute-start.7
  589.9 204.6 %scatter_custom_fusion.5 = f32[131072]{0:T(1024)S(1)} fusion(s32[32768]{0:T(1024)S(1)} %bitcast.77, f32[32768]{0:T(1024)S(1)} %bitcast_multiply_fusion.2, f32[]{:T(128)} %constant.8.clone.1), kind=kCustom, calls=%fused_computation.66 | custom fusion | flops 32768 | bytes 524292 | tf_op jit(solution)/shard_map/scatter-add | solution.py:72
  795.6 46.2 %psum.38 = f32[]{:T(128)} all-reduce(f32[]{:T(128)} %get-tuple-element.2), channel_id=1, replica_groups=mesh['lon'=4,'lat'=8] {'lon','lat'}, use_global_device_ids=true, to_apply=%region_18.19 | all-reduce | flops 1 | bytes 8 | tf_op jit(solution)/shard_map/psum | solution.py:89
  842.6 180.5 %gather_fusion.2 = f32[32768]{0:T(1024)S(1)} fusion(f32[131072]{0:T(1024)S(1)} %bitcast.72, s32[32768]{0:T(1024)S(1)} %fusion.32), kind=kCustom, calls=%fused_computation.2 | custom fusion | bytes 393216 | tf_op jit(solution)/shard_map/gather | solution.py:60
  1023.8 5.2 all-to-all-start.5
  1029.0 1.3 collective-permute-start.10
  1030.3 3.0 collective-permute-start.11
  1033.4 3.7 collective-permute-start.8
  1040.0 2.7 collective-permute-done.9
  1045.1 37.7 %psum.39 = f32[]{:T(128)} all-reduce(f32[]{:T(128)S(6)} %add.100), channel_id=1, replica_groups=mesh['lon'=4,'lat'=8] {'lon','lat'}, use_global_device_ids=true, to_apply=%region_23.24 | all-reduce | flops 1 | bytes 8 | tf_op jit(solution)/shard_map/psum | solution.py:84
  1083.8 180.5 %gather_fusion.4 = f32[32768]{0:T(1024)S(1)} fusion(f32[131072]{0:T(1024)S(1)} %bitcast.73, s32[32768]{0:T(1024)S(1)} %fusion.32), kind=kCustom, calls=%fused_computation.4 | custom fusion | bytes 393216 | tf_op jit(solution)/shard_map/gather | solution.py:60
  1264.5 12.9 %all_to_all.78 = f32[32,8,1]{1,2,0:T(1,128)S(1)} all-to-all(f32[32,8,1]{1,2,0:T(1,128)S(1)} %bitcast.79), channel_id=1, replica_groups=mesh['lon'=4,'lat'=8] {'lon','lat'}, dimensions={0} | all-to-all | bytes 2048 | tf_op jit(solution)/shard_map/all_to_all | solution.py:61
  (97 shorter events, 24.1 us)
Async XLA Ops:
  1.3 0.7 copy-start.5
  2.0 0.7 copy-start.4
  46.2 6.7 copy-start.1
  46.2 6.7 copy-start.2
  48.2 11.8 all-to-all-start.2
  60.0 2.7 copy-start.3
  60.0 10.9 all-to-all-start
  70.9 10.8 all-to-all-start.1
  513.3 13.2 %all-to-all-start.3 = ((f32[32,8,1]{1,2,0:T(1,128)}), f32[32,8,1]{1,2,0:T(1,128)S(1)}, u32[]{:S(2)}, u32[]{:S(2)}) async-start(f32[32,8,1]{1,2,0:T(1,128)} %bitcast.16), calls=%async_computation.3 | async-start | bytes 32768 | tf_op jit(solution)/shard_map/all_to_all | solution.py:61
  518.5 10.9 collective-permute-start.2
  519.8 9.6 collective-permute-start.3
  522.8 6.6 collective-permute-start
  526.5 5.6 collective-permute-start.1
  574.9 14.1 %all-to-all-start.4 = ((f32[32,8,1]{1,2,0:T(1,128)}), f32[32,8,1]{1,2,0:T(1,128)S(1)}, u32[]{:S(2)}, u32[]{:S(2)}) async-start(f32[32,8,1]{1,2,0:T(1,128)} %bitcast.20), calls=%async_computation.4 | async-start | bytes 32768 | tf_op jit(solution)/shard_map/all_to_all | solution.py:69
  581.0 213.6 %collective-permute-start.4 = (f32[1,32,128]{2,1,0:T(8,128)S(1)}, f32[1,32,128]{2,1,0:T(8,128)S(1)}, u32[]{:S(2)}, u32[]{:S(2)}) collective-permute-start(f32[1,32,128]{2,1,0:T(8,128)S(1)} %get-tuple-element.10), channel_id=1, source_target_pairs={{8,0},{16,8},{24,16},{0,24},{9,1},{17,9},{25,17},{1,25},{10,2},{18... | collective-permute-start | bytes 49160 | tf_op jit(solution)/shard_map/ppermute | solution.py:23
  584.6 209.9 %collective-permute-start.5 = (f32[1,32,128]{2,1,0:T(8,128)S(1)}, f32[1,32,128]{2,1,0:T(8,128)S(1)}, u32[]{:S(2)}, u32[]{:S(2)}) collective-permute-start(f32[1,32,128]{2,1,0:T(8,128)S(1)} %get-tuple-element.11), channel_id=1, source_target_pairs={{0,8},{8,16},{16,24},{24,0},{1,9},{9,17},{17,25},{25,1},{2,10},{10... | collective-permute-start | bytes 49160 | tf_op jit(solution)/shard_map/ppermute | solution.py:22
  584.6 209.9 %collective-permute-start.6 = (f32[32,1,128]{2,1,0:T(1,128)S(1)}, f32[32,1,128]{2,1,0:T(1,128)S(1)}, u32[]{:S(2)}, u32[]{:S(2)}) collective-permute-start(f32[32,1,128]{2,1,0:T(1,128)S(1)} %get-tuple-element.12), channel_id=1, source_target_pairs={{1,0},{2,1},{3,2},{4,3},{5,4},{6,5},{7,6},{9,8},{10,9},{11,10},{12... | collective-permute-start | bytes 49160 | tf_op jit(solution)/shard_map/ppermute | solution.py:23
  585.9 208.6 %collective-permute-start.7 = (f32[32,1,128]{2,1,0:T(1,128)S(1)}, f32[32,1,128]{2,1,0:T(1,128)S(1)}, u32[]{:S(2)}, u32[]{:S(2)}) collective-permute-start(f32[32,1,128]{2,1,0:T(1,128)S(1)} %get-tuple-element.13), channel_id=1, source_target_pairs={{0,1},{1,2},{2,3},{3,4},{4,5},{5,6},{6,7},{8,9},{9,10},{10,11},{11... | collective-permute-start | bytes 49160 | tf_op jit(solution)/shard_map/ppermute | solution.py:22
  1023.8 13.2 %all-to-all-start.5 = ((f32[32,8,1]{1,2,0:T(1,128)}), f32[32,8,1]{1,2,0:T(1,128)S(1)}, u32[]{:S(2)}, u32[]{:S(2)}) async-start(f32[32,8,1]{1,2,0:T(1,128)} %bitcast.26), calls=%async_computation.5 | async-start | bytes 32768 | tf_op jit(solution)/shard_map/all_to_all | solution.py:61
  1029.0 10.9 collective-permute-start.10
  1030.3 9.6 collective-permute-start.11
  1033.4 6.6 collective-permute-start.8
  1037.1 5.6 collective-permute-start.9
  1083.8 180.6 %copy-start = (f32[32,32,128]{2,1,0:T(8,128)}, f32[32,32,128]{2,1,0:T(8,128)S(1)}, u32[]{:S(2)}) copy-start(f32[32,32,128]{2,1,0:T(8,128)S(1)} %multiply_add_fusion) | copy-start | bytes 1572868
where the time goes:
time: 1280 us
  local copies, waits for them, and re-layouts  554 us (43%)
  other arithmetic  423 us (33%)
  blocking collectives  221 us (17%)
  starting transfers between devices  50.1 us (4%)
  waiting for transfers between devices  24.4 us (2%)
    gather x3, local copies, waits for them, and re-layouts, forward(): partial_value = jnp.sum(held_lens * cells[held_offs], axis=1)  542 us
    scatter-add x2, other arithmetic, backward(): jnp.zeros((brick_cells,), jnp.float32).at[held_offs.reshape(-1)]  409 us
    psum x3, blocking collectives, beta_total(): lax.psum(jnp.sum(ray_part * ray_part) + jnp.sum(grid_part * grid_part), (...  118 us
    psum x2, blocking collectives, alpha_total(): return lax.psum(jnp.sum(grid_part * grid_part), ('lon', 'lat'))  90.2 us
  transfers between devices with their start and end apart: 18, of which 5 were waited for; matrix products, arithmetic and copies ran while one was open for 17% of the time, Pallas kernels for 0%

commit v1 on v0

v1 whole, which is shorter than its diff:
```python
import jax
import jax.numpy as jnp
from jax import lax
from jax.experimental import pallas as pl
from jax.experimental.pallas import tpu as pltpu
from jax.sharding import PartitionSpec as P

CLON = 32
CLAT = 32
DEP = 128
COLS = CLON * CLAT
ROWS_M = COLS // 2
ROWS_N = 2 * DEP
CH = 8

damping = 0.01
AXES = ("lon", "lat")
f32 = jnp.float32
i32 = jnp.int32
bf16 = jnp.bfloat16
SM = pl.BlockSpec(memory_space=pltpu.SMEM)
VM = pl.BlockSpec(memory_space=pltpu.VMEM)


def iota(shape, dim):
    return lax.broadcasted_iota(i32, shape, dim)


def sds(shape, dtype=f32):
    return jax.ShapeDtypeStruct(shape, dtype)


def call(kernel, outs, ins, args, scratch=(), out_specs=None, name=None):
    return pl.pallas_call(
        kernel,
        out_shape=outs,
        in_specs=list(ins),
        out_specs=out_specs if out_specs is not None else [VM] * len(outs),
        scratch_shapes=list(scratch),
        name=name,
    )(*args)


def pack_kernel(devices, cap, rays, per_ray):
    width = 2 * cap + 1

    def kernel(brick, counts, times, offs, deps, lens, out, cells, used):
        lane = iota((1, 128), 1)
        out[...] = jnp.zeros_like(out)
        o = offs[...]
        cells[...] = ((o & (ROWS_M - 1)) * ROWS_N + (o >> 9) * DEP + deps[...]).astype(f32)

        def clear(d, carry):
            used[d] = 0
            return carry

        lax.fori_loop(0, devices, clear, 0)

        def one(r, row):
            value = times[r]
            for j in range(per_ray):
                b = brick[r, j]
                k = used[b]
                used[b] = k + 1
                base = b * width
                out[base + k] = cells[pl.ds(r * per_ray + j, 1), :]
                out[base + cap + k] = lens[pl.ds(r * per_ray + j, 1), :]
                extra = out[base + 2 * cap]
                extra = jnp.where(lane == k, r.astype(f32), extra)
                out[base + 2 * cap] = jnp.where(lane == 16 + k, value, extra)
            return jnp.where(lane == 64 + r, value, row)

        row = lax.fori_loop(0, counts[0], one, jnp.zeros((1, 128), f32))

        def finish(d, carry):
            at = d * width + 2 * cap
            extra = jnp.where(lane >= 64, row, out[at])
            out[at] = jnp.where(lane == 127, used[d].astype(f32), extra)
            return carry

        lax.fori_loop(0, devices, finish, 0)

    return kernel


def split(x):
    high = x.astype(bf16).astype(f32)
    return high, x - high


def lanes_of(block, i, n):
    return jnp.concatenate([block[i + j : i + j + 1, :] for j in range(n)], axis=1)


GROUP = 4


def scatter_tiles(total, cell_ref, w_ref, b_ref, acc):
    acc[...] = jnp.zeros_like(acc)
    seg = GROUP * 128
    im = iota((ROWS_M, seg), 0)
    inn = iota((ROWS_N, seg), 0)
    zero = jnp.zeros((), f32)

    def chunk(c, carry):
        at = pl.multiple_of(c * CH, CH)
        ci = cell_ref[pl.ds(at, CH), :].astype(i32)
        m = ci >> 8
        n = ci & (ROWS_N - 1)
        high, low = split(w_ref[pl.ds(at, CH), :] * b_ref[pl.ds(at, CH), :])
        for i in range(0, CH, GROUP):
            ohm = jnp.where(im == lanes_of(m, i, GROUP), 1.0, 0.0).astype(bf16)
            hit = inn == lanes_of(n, i, GROUP)
            vh = jnp.where(hit, lanes_of(high, i, GROUP), zero).astype(bf16)
            vl = jnp.where(hit, lanes_of(low, i, GROUP), zero).astype(bf16)
            dims = (((1,), (1,)), ((), ()))
            acc[...] += lax.dot_general(
                ohm, vh, dims, preferred_element_type=f32
            ) + lax.dot_general(ohm, vl, dims, preferred_element_type=f32)
        return carry

    lax.fori_loop(0, (total + CH - 1) // CH, chunk, 0)


def gather_tiles(total, cell_ref, w_ref, gh, gl, yv):
    yv[...] = jnp.zeros_like(yv)
    seg = 256
    im = iota((ROWS_M, seg), 0)
    inn = iota((ROWS_N, seg), 0)

    def chunk(c, carry):
        at = pl.multiple_of(c * CH, CH)
        ci = cell_ref[pl.ds(at, CH), :].astype(i32)
        m = ci >> 8
        n = ci & (ROWS_N - 1)
        rows = []
        for i in range(0, CH, 2):
            ohn = jnp.where(inn == lanes_of(n, i, 2), 1.0, 0.0).astype(bf16)
            full = jnp.dot(gh[...], ohn, preferred_element_type=f32) + jnp.dot(
                gl[...], ohn, preferred_element_type=f32
            )
            got = jnp.sum(jnp.where(im == lanes_of(m, i, 2), full, 0.0), axis=0, keepdims=True)
            rows += [got[:, :128], got[:, 128:]]
        yv[pl.ds(at, CH), :] = jnp.concatenate(rows, axis=0) * w_ref[pl.ds(at, CH), :]
        return carry

    lax.fori_loop(0, (total + CH - 1) // CH, chunk, 0)


def layers(src, lo, hi, la, lb):
    lo[...] = src[0:CLAT, :]
    hi[...] = src[COLS - CLAT : COLS, :]
    for i in range(CLON):
        la[i] = src[i * CLAT : i * CLAT + 1, :]
        lb[i] = src[(i + 1) * CLAT - 1 : (i + 1) * CLAT, :]


LAYERS = [(CLAT, DEP), (CLAT, DEP), (CLON, 1, DEP), (CLON, 1, DEP)]


def stencil_layer(i, src, before, after, lat_before, lat_after):
    sub = iota((CLAT, DEP), 0)
    lane = iota((CLAT, DEP), 1)
    c = src[i * CLAT : (i + 1) * CLAT, :]
    up = before[...] if i == 0 else src[(i - 1) * CLAT : i * CLAT, :]
    down = after[...] if i == CLON - 1 else src[(i + 1) * CLAT : (i + 2) * CLAT, :]
    lm = jnp.where(sub == 0, lat_before[i], pltpu.roll(c, 1, 0))
    lp = jnp.where(sub == CLAT - 1, lat_after[i], pltpu.roll(c, CLAT - 1, 0))
    dm = jnp.where(lane == 0, 0.0, pltpu.roll(c, 1, 1))
    dp = jnp.where(lane == DEP - 1, 0.0, pltpu.roll(c, DEP - 1, 1))
    return 6.0 * c - up - down - lm - lp - dm - dp


def colsum(x):
    return jnp.sum(x, axis=0, keepdims=True)


def start_kernel(devices, cap, rays):
    width = 2 * cap + 1

    def kernel(cnt, recv, g, lo, hi, la, lb, cell, w, q, data, total, b, acc):
        sub = iota((cap, 128), 0)
        lane = iota((cap, 128), 1)
        lane1 = iota((1, 128), 1)
        q[...] = jnp.full_like(q, -1.0)
        per_row = 128 // rays
        pos = 0
        row = jnp.zeros((1, 128), f32)
        for s in range(devices):
            at = s * width
            ext = recv[at + 2 * cap]
            wide = jnp.broadcast_to(ext, (cap, 128))
            qs = jnp.sum(jnp.where(lane == sub, wide, 0.0), axis=1, keepdims=True)
            bs = jnp.sum(jnp.where(lane == sub + 16, wide, 0.0), axis=1, keepdims=True)
            cell[pl.ds(pos, cap), :] = jnp.concatenate([recv[at + k] for k in range(cap)], axis=0)
            w[pl.ds(pos, cap), :] = jnp.concatenate(
                [recv[at + cap + k] for k in range(cap)], axis=0
            )
            q[pl.ds(pos, cap), :] = jnp.broadcast_to(qs + float(s * rays), (cap, 128))
            b[pl.ds(pos, cap), :] = jnp.broadcast_to(bs, (cap, 128))
            pos = pos + cnt[s]
            j = s % per_row
            moved = pltpu.roll(ext, (j * rays - 64) % 128, 1)
            inside = (lane1 >= j * rays) & (lane1 < (j + 1) * rays)
            row = jnp.where(inside, moved, row)
            if j == per_row - 1:
                data[s // per_row : s // per_row + 1, :] = row
        w[pl.ds(pos, CH), :] = jnp.zeros((CH, 128), f32)
        b[pl.ds(pos, CH), :] = jnp.zeros((CH, 128), f32)
        q[pl.ds(pos, CH), :] = jnp.full((CH, 128), -1.0, f32)
        total[0] = pos
        scatter_tiles(pos, cell, w, b, acc)
        g[0:ROWS_M, :] = acc[:, :DEP]
        g[ROWS_M:COLS, :] = acc[:, DEP:]
        layers(g, lo, hi, la, lb)

    return kernel


def ray_onehots(q):
    qi = q[...].astype(i32)
    lane = iota(qi.shape, 1)
    return jnp.where((qi >> 7) == lane, 1.0, 0.0), (qi & 127) == lane


def forward_kernel(ray_rows):
    def kernel(total, src, cell, w, q, y, gh, gl, yv):
        for half in range(2):
            rows = slice(half * ROWS_M, (half + 1) * ROWS_M)
            cols = slice(half * DEP, (half + 1) * DEP)
            high, low = split(src[rows, :])
            gh[:, cols] = high.astype(bf16)
            gl[:, cols] = low.astype(bf16)
        gather_tiles(total[0], cell, w, gh, gl, yv)
        oh, ql = ray_onehots(q)
        ys = jnp.where(ql, jnp.sum(yv[...], axis=1, keepdims=True), 0.0)
        full = lax.dot_general(
            oh,
            ys,
            (((0,), (0,)), ((), ())),
            precision=lax.Precision.HIGHEST,
            preferred_element_type=f32,
        )
        y[...] = full[:ray_rows, :]

    return kernel


def send_copies(out, devices, rows):
    count = len(rows)

    def one(d, carry):
        for i, row in enumerate(rows):
            out[d * count + i] = row
        return carry

    lax.fori_loop(0, devices, one, 0)


def smooth_kernel(devices, ray_rows):
    def kernel(g, before, after, lat_before, lat_after, y, q1, lo, hi, la, lb, out):
        gg = jnp.zeros((CLAT, DEP), f32)
        qq = jnp.zeros((CLAT, DEP), f32)
        for i in range(CLON):
            res = stencil_layer(i, g, before, after, lat_before, lat_after)
            q1[i * CLAT : (i + 1) * CLAT, :] = res
            c = g[i * CLAT : (i + 1) * CLAT, :]
            gg = gg + c * c
            qq = qq + res * res
        layers(q1, lo, hi, la, lb)
        rows = [y[i : i + 1, :] for i in range(ray_rows)] + [colsum(gg), colsum(qq)]
        send_copies(out, devices, rows)

    return kernel


def received(recv, devices, count):
    def one(d, acc):
        return acc + recv[pl.ds(d * count, count)]

    return lax.fori_loop(0, devices, one, jnp.zeros((count, 1, 128), f32))


def all_rows(acc, start, count):
    return jnp.concatenate([acc[start + i] for i in range(count)], axis=0)


def total_of(x):
    return jnp.sum(jnp.sum(x, axis=0, keepdims=True), axis=1, keepdims=True)


def first_scalars(recv, data, devices, ray_rows):
    acc = received(recv, devices, ray_rows + 2)
    p1 = all_rows(acc, 0, ray_rows)
    gg = total_of(acc[ray_rows])
    qq = total_of(acc[ray_rows + 1])
    beta1 = jnp.sqrt(total_of(data * data))
    nrm = jnp.sqrt(gg)
    alpha1 = nrm / beta1
    av1 = p1 / nrm
    r2 = av1 - alpha1 * (data / beta1)
    beta2 = jnp.sqrt(total_of(r2 * r2) + (damping * damping) * (qq / gg))
    return av1, r2 / beta2, nrm, beta1, alpha1, beta2, qq


def second_kernel(devices, ray_rows):
    def kernel(
        total, recv, data, g, q1, before, after, lat_before, lat_after, cell, w, q,
        v, lo, hi, la, lb, av, u2, num, b, acc,
    ):
        av1, u, nrm, beta1, alpha1, beta2, qq = first_scalars(recv, data[...], devices, ray_rows)
        av[...] = av1
        u2[...] = u
        numbers = [nrm, beta1, alpha1, beta2, qq]
        lane = iota((1, 128), 1)
        packed = jnp.zeros((1, 128), f32)
        for i, x in enumerate(numbers):
            packed = jnp.where(lane == i, x, packed)
        num[...] = packed
        oh, ql = ray_onehots(q)
        padded = jnp.concatenate([u, jnp.zeros((128 - ray_rows, 128), f32)], axis=0)
        picked = jnp.dot(oh, padded, precision=lax.Precision.HIGHEST, preferred_element_type=f32)
        picked = jnp.sum(jnp.where(ql, picked, 0.0), axis=1, keepdims=True)
        b[...] = jnp.broadcast_to(picked, b.shape)
        scatter_tiles(total[0], cell, w, b, acc)
        a = (damping * damping) / (nrm * beta2)
        e = beta2 / nrm
        for i in range(CLON):
            half, at = divmod(i * CLAT, ROWS_M)
            h = acc[at : at + CLAT, half * DEP : (half + 1) * DEP]
            res = stencil_layer(i, q1, before, after, lat_before, lat_after)
            v[i * CLAT : (i + 1) * CLAT, :] = h + a * res - e * g[i * CLAT : (i + 1) * CLAT, :]
        layers(v, lo, hi, la, lb)

    return kernel


def last_smooth_kernel(devices, ray_rows):
    def kernel(v, q1, before, after, lat_before, lat_after, y, out):
        vv = jnp.zeros((CLAT, DEP), f32)
        ll = jnp.zeros((CLAT, DEP), f32)
        lq = jnp.zeros((CLAT, DEP), f32)
        for i in range(CLON):
            res = stencil_layer(i, v, before, after, lat_before, lat_after)
            c = v[i * CLAT : (i + 1) * CLAT, :]
            vv = vv + c * c
            ll = ll + res * res
            lq = lq + res * q1[i * CLAT : (i + 1) * CLAT, :]
        rows = [y[i : i + 1, :] for i in range(ray_rows)] + [colsum(vv), colsum(ll), colsum(lq)]
        send_copies(out, devices, rows)

    return kernel


def final_kernel(devices, ray_rows, rays):
    def kernel(me, recv, data, av, u2, num, g, v, model, misfit):
        acc = received(recv, devices, ray_rows + 3)
        p2 = all_rows(acc, 0, ray_rows)
        vv = total_of(acc[ray_rows])
        ll = total_of(acc[ray_rows + 1])
        lq = total_of(acc[ray_rows + 2])
        nrm, beta1, alpha1, beta2, qq = [num[0:1, i : i + 1] for i in range(5)]
        alpha2 = jnp.sqrt(vv)
        av2 = p2 / alpha2
        r3 = av2 - alpha2 * u2[...]
        x = alpha2 / (nrm * beta2)
        grid = ll / vv - 2.0 * (x / alpha2) * lq + (x * x) * qq
        beta3sq = total_of(r3 * r3) + (damping * damping) * grid
        rho = jnp.sqrt(alpha1 * alpha1 + beta2 * beta2)
        cosine = alpha1 / rho
        sine = beta2 / rho
        theta = sine * alpha2
        rho_bar = -cosine * alpha2
        k1 = cosine * beta1 / rho
        t = theta / rho
        phi_bar = sine * beta1
        rho2 = jnp.sqrt(rho_bar * rho_bar + beta3sq)
        k2 = (rho_bar / rho2) * phi_bar / rho2
        first = k1 - k2 * t
        model[...] = (first / nrm) * g[...] + (k2 / alpha2) * v[...]
        mis = data[...] - (first * av[...] + k2 * av2)
        per_row = 128 // rays
        d = me[0]
        sub = iota(mis.shape, 0)
        mine = colsum(jnp.where(sub == d // per_row, mis, 0.0))
        misfit[...] = pltpu.roll(mine, (128 - (d % per_row) * rays) % 128, 1)

    return kernel


def exchange_all(x):
    return lax.all_to_all(x, AXES, split_axis=0, concat_axis=0, tiled=True)


def halo(parts):
    lo, hi, la, lb = parts

    def ring(axis, wrap):
        n = lax.axis_size(axis)
        up = [(i, (i + 1) % n) for i in range(n if wrap else n - 1)]
        return up, [(j, i) for i, j in up]

    up, down = ring("lon", True)
    lat_up, lat_down = ring("lat", False)
    return (
        lax.ppermute(hi, "lon", up),
        lax.ppermute(lo, "lon", down),
        lax.ppermute(lb, "lat", lat_up),
        lax.ppermute(la, "lat", lat_down),
    )


def shards(travel_times, ray_counts, tile_brick, cell_offsets, cell_depths, seg_lengths):
    devices = lax.axis_size(AXES)
    rays, per_ray, segs = cell_offsets.shape
    tiles = rays * per_ray
    slots = 2 * tiles
    cap = slots // devices
    width = 2 * cap + 1
    ray_rows = devices * rays // 128
    room = slots + CH
    flat = lambda x: x.reshape(tiles, segs)
    layer_outs = [sds(s) for s in LAYERS]
    grid = sds((COLS, DEP))
    buf = lambda dtype: pltpu.VMEM((ROWS_M, ROWS_N), dtype)

    (packed,) = call(
        pack_kernel(devices, cap, rays, per_ray),
        [sds((devices * width, 1, 128))],
        [SM, SM, SM, VM, VM, VM],
        (tile_brick, ray_counts, travel_times, flat(cell_offsets), flat(cell_depths), flat(seg_lengths)),
        [pltpu.VMEM((tiles, segs), f32), pltpu.SMEM((devices,), i32)],
        name="pack",
    )
    recv0 = exchange_all(packed)
    counts = recv0.reshape(devices, width, 128)[:, 2 * cap, 127].astype(i32)
    g, *edges, cell, w, q, data, total = call(
        start_kernel(devices, cap, rays),
        [grid, *layer_outs, sds((room, 128)), sds((room, 128)), sds((room, 128)), sds((ray_rows, 128)), sds((1,), i32)],
        [SM, VM],
        (counts, recv0),
        [pltpu.VMEM((room, 128), f32), buf(f32)],
        out_specs=[VM] * 9 + [SM],
        name="start",
    )
    gather_scratch = [buf(bf16), buf(bf16), pltpu.VMEM((room, 128), f32)]
    around = halo(edges)
    (y1,) = call(
        forward_kernel(ray_rows), [sds((ray_rows, 128))], [SM] + [VM] * 4, (total, g, cell, w, q),
        gather_scratch, name="forward",
    )
    q1, *edges, send = call(
        smooth_kernel(devices, ray_rows),
        [grid, *layer_outs, sds((devices * (ray_rows + 2), 1, 128))],
        [VM] * 6,
        (g, *around, y1),
        name="smooth",
    )
    around = halo(edges)
    recv1 = exchange_all(send)
    v, *edges, av, u2, num = call(
        second_kernel(devices, ray_rows),
        [grid, *layer_outs, sds((ray_rows, 128)), sds((ray_rows, 128)), sds((1, 128))],
        [SM] + [VM] * 11,
        (total, recv1, data, g, q1, *around, cell, w, q),
        [pltpu.VMEM((room, 128), f32), buf(f32)],
        name="second",
    )
    around = halo(edges)
    (y2,) = call(
        forward_kernel(ray_rows), [sds((ray_rows, 128))], [SM] + [VM] * 4, (total, v, cell, w, q),
        gather_scratch, name="forward",
    )
    (send,) = call(
        last_smooth_kernel(devices, ray_rows),
        [sds((devices * (ray_rows + 3), 1, 128))],
        [VM] * 7,
        (v, q1, *around, y2),
        name="last_smooth",
    )
    recv2 = exchange_all(send)
    me = lax.axis_index(AXES).astype(i32).reshape(1)
    model, mis = call(
        final_kernel(devices, ray_rows, rays),
        [grid, sds((1, 128))],
        [SM] + [VM] * 7,
        (me, recv2, data, av, u2, num, g, v),
        name="final",
    )
    return model.reshape(CLON, CLAT, DEP), mis[0, :rays]


def solution(mesh):
    placed = (
        P(("lon", "lat")),
        P(("lon", "lat")),
        P(("lon", "lat"), None),
        P(("lon", "lat"), None, None),
        P(("lon", "lat"), None, None),
        P(("lon", "lat"), None, None),
    )
    return jax.shard_map(
        shards,
        mesh=mesh,
        in_specs=placed,
        out_specs=(P("lon", "lat", None), P(("lon", "lat"))),
        check_vma=False,
    )
```

time: 1280 us -> 152 us (0.12)
  local copies, waits for them, and re-layouts: 554 us -> 6.17 us
  other arithmetic: 423 us -> 2.55 us
  blocking collectives: 221 us -> 18.1 us
  Pallas kernels: 0 us -> 45.9 us
    gather x6 -> x0, local copies, waits for them, and re-layouts: 545 us -> none  [the longest x3 542 us: forward(): partial_value = jnp.sum(held_lens * cells[held_offs], axis=1)]
    scatter-add x2 -> x0, other arithmetic: 409 us -> none  [backward(): jnp.zeros((brick_cells,), jnp.float32).at[held_offs.reshape(-1)]]
    psum x5 -> x0, blocking collectives: 208 us -> none  [the longest x3 118 us: beta_total(): lax.psum(jnp.sum(ray_part * ray_part) + jnp.sum(grid_part * grid_part), (...]
    pallas_call x0 -> x8, Pallas kernels: none -> 45.9 us  [call(): pl.pallas_call(kernel, out_shape=outs, in_specs=list(ins), out_specs=out_...]
    all_to_all x6 -> x2, starting transfers between devices: 26.1 us -> 40.3 us  [exchange_all(): return lax.all_to_all(x, AXES, split_axis=0, concat_axis=0, tiled=True)]
  transfers between devices with their start and end apart: 18 -> 14, of which waited for: 5 -> 4; matrix products, arithmetic and copies ran while one was open for 17% -> 0% of each run, Pallas kernels for 0% -> 11%
where the time goes in v1:
time: 152 us; the launch traced here: 151 us
  starting transfers between devices  62.2 us (41%)
  Pallas kernels  45.9 us (30%)
  blocking collectives  18.1 us (12%)
  waiting for transfers between devices  14.5 us (10%)
  local copies, waits for them, and re-layouts  6.17 us (4%)
  other arithmetic  2.55 us (2%)
  between operations  1.55 us (1%)
    pallas_call x8, Pallas kernels, call(): pl.pallas_call(kernel, out_shape=outs, in_specs=list(ins), out_specs=out_...  45.9 us
    all_to_all x2, starting transfers between devices, exchange_all(): return lax.all_to_all(x, AXES, split_axis=0, concat_axis=0, tiled=True)  40.3 us
    all_to_all x1, blocking collectives, exchange_all(): return lax.all_to_all(x, AXES, split_axis=0, concat_axis=0, tiled=True)  18.1 us
    all_to_all x2, waiting for transfers between devices, exchange_all(): return lax.all_to_all(x, AXES, split_axis=0, concat_axis=0, tiled=True)  8.79 us
    ppermute x3, starting transfers between devices, halo(): lax.ppermute(lo, 'lon', down)  7.52 us
    ppermute x3, starting transfers between devices, halo(): lax.ppermute(lb, 'lat', lat_up)  6.44 us
    unnamed x41, local copies, waits for them, and re-layouts  5.09 us
    ppermute x3, waiting for transfers between devices, halo(): lax.ppermute(la, 'lat', lat_down)  4.61 us
  transfers between devices with their start and end apart: 14, of which 4 were waited for; matrix products, arithmetic and copies ran while one was open for 0% of the time, Pallas kernels for 11%

profile of v1, /device:TPU:0, one launch (start us, length us, event | category | flops | bytes accessed | tf_op | source)
XLA Modules:
  0.0 151.0 jit_solution(12482142172264708698)
XLA Ops:
  0.6 1.4 copy.11.brick
  2.6 3.2 %pack.1 = f32[544,1,128]{2,1,0:T(1,128)} custom-call(s32[32,4]{1,0:T(8,128)} %copy.11.brick, s32[1]{0:T(128)S(6)} %copy.16.counts, f32[32]{0:T(128)} %times.1, s32[128,128]{1,0:T(8,128)} %bitcast.8, s32[128,128]{1,0:T(8,128)} %bitcast.9, f32[128,128]{1,0:T(8,128)} %bitcast.10), custom_call_target="tpu_custom_call" | custom-call | tf_op jit(solution)/shard_map/pack/pallas_call | solution.py:34
  5.9 18.1 %all_to_all.15.recv = f32[544,1,128]{2,1,0:T(1,128)S(1)} all-to-all(f32[544,1,128]{2,1,0:T(1,128)} %pack.1), channel_id=1, replica_groups=mesh['lon'=4,'lat'=8] {'lon','lat'}, dimensions={0} | all-to-all | bytes 557056 | tf_op jit(solution)/shard_map/all_to_all | solution.py:392
  24.6 1.3 reduce.5
  25.9 1.3 fusion.cnt
  27.2 8.3 %start.1 = (f32[1024,128]{1,0:T(8,128)}, f32[32,128]{1,0:T(8,128)}, f32[32,128]{1,0:T(8,128)}, f32[32,1,128]{2,1,0:T(1,128)}, f32[32,1,128]{2,1,0:T(1,128)}, /*i...) custom-call(s32[32]{0:T(128)} %fusion.cnt, f32[544,1,128]{2,1,0:T(1,128)} %copy-done), custom_call_target="tpu_custom_call" | custom-call | tf_op jit(solution)/shard_map/start/pallas_call | solution.py:34
  35.5 3.8 %collective-permute-start.1 = (f32[32,128]{1,0:T(8,128)}, f32[32,128]{1,0:T(8,128)S(1)}, u32[]{:S(2)}, u32[]{:S(2)}) collective-permute-start(f32[32,128]{1,0:T(8,128)} %get-tuple-element.31), channel_id=1, source_target_pairs={{8,0},{16,8},{24,16},{0,24},{9,1},{17,9},{25,17},{1,25},{10,2},{18... | collective-permute-start | bytes 49160 | tf_op jit(solution)/shard_map/ppermute | solution.py:407
  39.3 1.3 collective-permute-start.2
  40.6 1.3 collective-permute-start.3
  41.9 8.4 %forward.2.y = f32[8,128]{1,0:T(8,128)} custom-call(s32[1]{0:T(128)} %get-tuple-element.28.total, f32[1024,128]{1,0:T(8,128)} %get-tuple-element.29.src.g, f32[264,128]{1,0:T(8,128)} %get-tuple-element.34.cell, f32[264,128]{1,0:T(8,128)} %get-tuple-element.35.w, f32[264,128]{1,0:T(8,128)} %get-tuple-element.36.q), custom_call_target="tpu_custom_call" | custom-call | tf_op jit(solution)/shard_map/forward/pallas_call | solution.py:34
  50.3 2.2 %collective-permute-done.3.lat_after = f32[32,1,128]{2,1,0:T(1,128)S(1)} collective-permute-done((f32[32,1,128]{2,1,0:T(1,128)}, f32[32,1,128]{2,1,0:T(1,128)S(1)}, u32[]{:S(2)}, u32[]{:S(2)}) %collective-permute-start.3) | collective-permute-done | bytes 16416 | tf_op jit(solution)/shard_map/ppermute | solution.py:409
  53.1 2.6 %smooth.1 = (f32[1024,128]{1,0:T(8,128)}, f32[32,128]{1,0:T(8,128)}, f32[32,128]{1,0:T(8,128)}, f32[32,1,128]{2,1,0:T(1,128)}, f32[32,1,128]{2,1,0:T(1,128)}, /*index=5*/f32[320,1,128]{2,1,0:T(1,128)}) custom-call(f32[1024,128]{1,0:T(8,128)} %get-tuple-element.29.src.g, f32[32,128]{1,0:T(8,128)} %copy-done.11, f32[32,128]{1,0:T(8,128)} %copy-done.12, ...), custom_call_target="tpu_custom_call" | custom-call | tf_op jit(solution)/shard_map/smooth/pallas_call | solution.py:34
  55.7 19.0 %all-to-all-start.1 = ((f32[320,1,128]{2,1,0:T(1,128)}), f32[320,1,128]{2,1,0:T(1,128)S(1)}, u32[]{:S(2)}, u32[]{:S(2)}) async-start(f32[320,1,128]{2,1,0:T(1,128)} %get-tuple-element.37), calls=%async_computation.1 | async-start | bytes 327680 | tf_op jit(solution)/shard_map/all_to_all | solution.py:392
  74.7 1.8 %collective-permute-start.4 = (f32[32,128]{1,0:T(8,128)S(1)}, f32[32,128]{1,0:T(8,128)S(1)}, u32[]{:S(2)}, u32[]{:S(2)}) collective-permute-start(f32[32,128]{1,0:T(8,128)S(1)} %copy-done.18), channel_id=1, source_target_pairs={{0,8},{8,16},{16,24},{24,0},{1,9},{9,17},{17,25},{25,1},{2,10},{10... | collective-permute-start | bytes 49160 | tf_op jit(solution)/shard_map/ppermute | solution.py:406
  76.5 2.1 %collective-permute-start.5 = (f32[32,128]{1,0:T(8,128)S(1)}, f32[32,128]{1,0:T(8,128)S(1)}, u32[]{:S(2)}, u32[]{:S(2)}) collective-permute-start(f32[32,128]{1,0:T(8,128)S(1)} %copy-done.17), channel_id=1, source_target_pairs={{8,0},{16,8},{24,16},{0,24},{9,1},{17,9},{25,17},{1,25},{10,2},{18... | collective-permute-start | bytes 49160 | tf_op jit(solution)/shard_map/ppermute | solution.py:407
  78.6 1.6 %collective-permute-start.6 = (f32[32,1,128]{2,1,0:T(1,128)S(1)}, f32[32,1,128]{2,1,0:T(1,128)S(1)}, u32[]{:S(2)}, u32[]{:S(2)}) collective-permute-start(f32[32,1,128]{2,1,0:T(1,128)S(1)} %copy-done.16), channel_id=1, source_target_pairs={{0,1},{1,2},{2,3},{3,4},{4,5},{5,6},{6,7},{8,9},{9,10},{10,11},{11... | collective-permute-start | bytes 49160 | tf_op jit(solution)/shard_map/ppermute | solution.py:408
  80.2 1.3 collective-permute-start.7
  81.5 1.0 collective-permute-done.4.before
  82.6 2.4 %collective-permute-done.7.lat_after = f32[32,1,128]{2,1,0:T(1,128)S(1)} collective-permute-done((f32[32,1,128]{2,1,0:T(1,128)S(1)}, f32[32,1,128]{2,1,0:T(1,128)S(1)}, u32[]{:S(2)}, u32[]{:S(2)}) %collective-permute-start.7) | collective-permute-done | bytes 16416 | tf_op jit(solution)/shard_map/ppermute | solution.py:409
  85.7 9.9 %second.1 = (f32[1024,128]{1,0:T(8,128)}, f32[32,128]{1,0:T(8,128)}, f32[32,128]{1,0:T(8,128)}, f32[32,1,128]{2,1,0:T(1,128)}, f32[32,1,128]{2,1,0:T(1,128)}, /*...) custom-call(s32[1]{0:T(128)} %get-tuple-element.28.total, f32[320,1,128]{2,1,0:T(1,128)} %copy-done.2, ...), custom_call_target="tpu_custom_call" | custom-call | tf_op jit(solution)/shard_map/second/pallas_call | solution.py:34
  95.5 3.6 %collective-permute-start.10 = (f32[32,1,128]{2,1,0:T(1,128)}, f32[32,1,128]{2,1,0:T(1,128)S(1)}, u32[]{:S(2)}, u32[]{:S(2)}) collective-permute-start(f32[32,1,128]{2,1,0:T(1,128)} %get-tuple-element.47), channel_id=1, source_target_pairs={{0,1},{1,2},{2,3},{3,4},{4,5},{5,6},{6,7},{8,9},{9,10},{10,11},{11... | collective-permute-start | bytes 49160 | tf_op jit(solution)/shard_map/ppermute | solution.py:408
  99.1 1.3 collective-permute-start.11
  100.4 2.2 %collective-permute-start.8 = (f32[32,128]{1,0:T(8,128)}, f32[32,128]{1,0:T(8,128)S(1)}, u32[]{:S(2)}, u32[]{:S(2)}) collective-permute-start(f32[32,128]{1,0:T(8,128)} %get-tuple-element.45), channel_id=1, source_target_pairs={{0,8},{8,16},{16,24},{24,0},{1,9},{9,17},{17,25},{25,1},{2,10},{10... | collective-permute-start | bytes 49160 | tf_op jit(solution)/shard_map/ppermute | solution.py:406
  102.6 1.7 %collective-permute-start.9 = (f32[32,128]{1,0:T(8,128)}, f32[32,128]{1,0:T(8,128)S(1)}, u32[]{:S(2)}, u32[]{:S(2)}) collective-permute-start(f32[32,128]{1,0:T(8,128)} %get-tuple-element.46), channel_id=1, source_target_pairs={{8,0},{16,8},{24,16},{0,24},{9,1},{17,9},{25,17},{1,25},{10,2},{18... | collective-permute-start | bytes 49160 | tf_op jit(solution)/shard_map/ppermute | solution.py:407
  104.3 8.4 %forward.3.y = f32[8,128]{1,0:T(8,128)} custom-call(s32[1]{0:T(128)} %get-tuple-element.28.total, f32[1024,128]{1,0:T(8,128)} %get-tuple-element.44.src.v, f32[264,128]{1,0:T(8,128)} %get-tuple-element.34.cell, f32[264,128]{1,0:T(8,128)} %get-tuple-element.35.w, f32[264,128]{1,0:T(8,128)} %get-tuple-element.36.q), custom_call_target="tpu_custom_call" | custom-call | tf_op jit(solution)/shard_map/forward/pallas_call | solution.py:34
  113.3 0.6 copy-done.10
  113.9 2.4 %last_smooth.1 = f32[352,1,128]{2,1,0:T(1,128)} custom-call(f32[1024,128]{1,0:T(8,128)} %get-tuple-element.44.src.v, f32[1024,128]{1,0:T(8,128)} %get-tuple-element.39.q1, f32[32,128]{1,0:T(8,128)} %copy-done.9, f32[32,128]{1,0:T(8,128)} %copy-done.10, f32[32,1,128]{2,1,0:T(1,128)} %copy-done.7, f32[32,1,128]{2,1,0:T(1,128)} %copy-done.8, f32[8,128]{1,0:T(8,128)} %forward.3.y), custom_call_target="tpu_custom_call" | custom-call | tf_op jit(solution)/shard_map/last_smooth/pallas_call | solution.py:34
  116.3 21.3 %all-to-all-start.2 = ((f32[352,1,128]{2,1,0:T(1,128)}), f32[352,1,128]{2,1,0:T(1,128)S(1)}, u32[]{:S(2)}, u32[]{:S(2)}) async-start(f32[352,1,128]{2,1,0:T(1,128)} %last_smooth.1), calls=%async_computation.2 | async-start | bytes 360448 | tf_op jit(solution)/shard_map/all_to_all | solution.py:392
  137.7 8.8 %all-to-all-done.2.recv = f32[352,1,128]{2,1,0:T(1,128)S(1)} async-done(((f32[352,1,128]{2,1,0:T(1,128)}), f32[352,1,128]{2,1,0:T(1,128)S(1)}, u32[]{:S(2)}, u32[]{:S(2)}) %all-to-all-start.2) | async-done | bytes 180256 | tf_op jit(solution)/shard_map/all_to_all | solution.py:392
  146.5 0.7 copy-done.1
  147.1 2.7 %final.1 = (f32[1024,128]{1,0:T(8,128)}, f32[1,128]{1,0:T(1,128)}) custom-call(s32[1]{0:T(128)} %bitcast.me, f32[352,1,128]{2,1,0:T(1,128)} %copy-done.1, f32[8,128]{1,0:T(8,128)} %get-tuple-element.38.data, f32[8,128]{1,0:T(8,128)} %get-tuple-element.49.av, f32[8,128]{1,0:T(8,128)} %get-tuple-element.50.u2, f32[1,128]{1,0:T(1,128)} %get-tuple-element.51.num, ...), custom_call_target="tpu_custom_call" | custom-call | tf_op jit(solution)/shard_map/final/pallas_call | solution.py:34
  149.9 0.6 copy-done.19
  (51 shorter events, 3.0 us)
Async XLA Ops:
  24.0 1.8 %copy-start = (f32[544,1,128]{2,1,0:T(1,128)}, f32[544,1,128]{2,1,0:T(1,128)S(1)}, u32[]{:S(2)}) copy-start(f32[544,1,128]{2,1,0:T(1,128)S(1)} %all_to_all.15.recv) | copy-start | bytes 835588
  35.4 14.9 %collective-permute-start = (f32[32,128]{1,0:T(8,128)}, f32[32,128]{1,0:T(8,128)S(1)}, u32[]{:S(2)}, u32[]{:S(2)}) collective-permute-start(f32[32,128]{1,0:T(8,128)} %get-tuple-element.30), channel_id=1, source_target_pairs={{0,8},{8,16},{16,24},{24,0},{1,9},{9,17},{17,25},{25,1},{2,10},{10... | collective-permute-start | bytes 49160 | tf_op jit(solution)/shard_map/ppermute | solution.py:406
  35.5 14.8 %collective-permute-start.1 = (f32[32,128]{1,0:T(8,128)}, f32[32,128]{1,0:T(8,128)S(1)}, u32[]{:S(2)}, u32[]{:S(2)}) collective-permute-start(f32[32,128]{1,0:T(8,128)} %get-tuple-element.31), channel_id=1, source_target_pairs={{8,0},{16,8},{24,16},{0,24},{9,1},{17,9},{25,17},{1,25},{10,2},{18... | collective-permute-start | bytes 49160 | tf_op jit(solution)/shard_map/ppermute | solution.py:407
  39.3 11.0 %collective-permute-start.2 = (f32[32,1,128]{2,1,0:T(1,128)}, f32[32,1,128]{2,1,0:T(1,128)S(1)}, u32[]{:S(2)}, u32[]{:S(2)}) collective-permute-start(f32[32,1,128]{2,1,0:T(1,128)} %get-tuple-element.32), channel_id=1, source_target_pairs={{0,1},{1,2},{2,3},{3,4},{4,5},{5,6},{6,7},{8,9},{9,10},{10,11},{11... | collective-permute-start | bytes 49160 | tf_op jit(solution)/shard_map/ppermute | solution.py:408
  40.6 11.9 %collective-permute-start.3 = (f32[32,1,128]{2,1,0:T(1,128)}, f32[32,1,128]{2,1,0:T(1,128)S(1)}, u32[]{:S(2)}, u32[]{:S(2)}) collective-permute-start(f32[32,1,128]{2,1,0:T(1,128)} %get-tuple-element.33), channel_id=1, source_target_pairs={{1,0},{2,1},{3,2},{4,3},{5,4},{6,5},{7,6},{9,8},{10,9},{11,10},{12... | collective-permute-start | bytes 49160 | tf_op jit(solution)/shard_map/ppermute | solution.py:409
  50.3 2.3 %copy-start.11 = (f32[32,128]{1,0:T(8,128)}, f32[32,128]{1,0:T(8,128)S(1)}, u32[]{:S(2)}) copy-start(f32[32,128]{1,0:T(8,128)S(1)} %collective-permute-done.before) | copy-start | bytes 49156
  50.3 2.2 %copy-start.12 = (f32[32,128]{1,0:T(8,128)}, f32[32,128]{1,0:T(8,128)S(1)}, u32[]{:S(2)}) copy-start(f32[32,128]{1,0:T(8,128)S(1)} %collective-permute-done.1.after) | copy-start | bytes 49156
  50.3 2.2 %copy-start.13 = (f32[32,1,128]{2,1,0:T(1,128)}, f32[32,1,128]{2,1,0:T(1,128)S(1)}, u32[]{:S(2)}) copy-start(f32[32,1,128]{2,1,0:T(1,128)S(1)} %collective-permute-done.2.lat_before) | copy-start | bytes 49156
  52.5 0.6 copy-start.14
  55.7 19.0 %copy-start.18 = (f32[32,128]{1,0:T(8,128)S(1)}, f32[32,128]{1,0:T(8,128)}, u32[]{:S(2)}) copy-start(f32[32,128]{1,0:T(8,128)} %get-tuple-element.40) | copy-start | bytes 49156
  55.7 20.8 %copy-start.17 = (f32[32,128]{1,0:T(8,128)S(1)}, f32[32,128]{1,0:T(8,128)}, u32[]{:S(2)}) copy-start(f32[32,128]{1,0:T(8,128)} %get-tuple-element.41) | copy-start | bytes 49156
  55.7 22.9 %copy-start.16 = (f32[32,1,128]{2,1,0:T(1,128)S(1)}, f32[32,1,128]{2,1,0:T(1,128)}, u32[]{:S(2)}) copy-start(f32[32,1,128]{2,1,0:T(1,128)} %get-tuple-element.42) | copy-start | bytes 49156
  55.7 24.5 %copy-start.15 = (f32[32,1,128]{2,1,0:T(1,128)S(1)}, f32[32,1,128]{2,1,0:T(1,128)}, u32[]{:S(2)}) copy-start(f32[32,1,128]{2,1,0:T(1,128)} %get-tuple-element.43) | copy-start | bytes 49156
  55.7 29.3 %all-to-all-start.1 = ((f32[320,1,128]{2,1,0:T(1,128)}), f32[320,1,128]{2,1,0:T(1,128)S(1)}, u32[]{:S(2)}, u32[]{:S(2)}) async-start(f32[320,1,128]{2,1,0:T(1,128)} %get-tuple-element.37), calls=%async_computation.1 | async-start | bytes 327680 | tf_op jit(solution)/shard_map/all_to_all | solution.py:392
  74.7 7.8 %collective-permute-start.4 = (f32[32,128]{1,0:T(8,128)S(1)}, f32[32,128]{1,0:T(8,128)S(1)}, u32[]{:S(2)}, u32[]{:S(2)}) collective-permute-start(f32[32,128]{1,0:T(8,128)S(1)} %copy-done.18), channel_id=1, source_target_pairs={{0,8},{8,16},{16,24},{24,0},{1,9},{9,17},{17,25},{25,1},{2,10},{10... | collective-permute-start | bytes 49160 | tf_op jit(solution)/shard_map/ppermute | solution.py:406
  76.5 6.0 %collective-permute-start.5 = (f32[32,128]{1,0:T(8,128)S(1)}, f32[32,128]{1,0:T(8,128)S(1)}, u32[]{:S(2)}, u32[]{:S(2)}) collective-permute-start(f32[32,128]{1,0:T(8,128)S(1)} %copy-done.17), channel_id=1, source_target_pairs={{8,0},{16,8},{24,16},{0,24},{9,1},{17,9},{25,17},{1,25},{10,2},{18... | collective-permute-start | bytes 49160 | tf_op jit(solution)/shard_map/ppermute | solution.py:407
  78.6 4.0 %collective-permute-start.6 = (f32[32,1,128]{2,1,0:T(1,128)S(1)}, f32[32,1,128]{2,1,0:T(1,128)S(1)}, u32[]{:S(2)}, u32[]{:S(2)}) collective-permute-start(f32[32,1,128]{2,1,0:T(1,128)S(1)} %copy-done.16), channel_id=1, source_target_pairs={{0,1},{1,2},{2,3},{3,4},{4,5},{5,6},{6,7},{8,9},{9,10},{10,11},{11... | collective-permute-start | bytes 49160 | tf_op jit(solution)/shard_map/ppermute | solution.py:408
  80.2 4.8 %collective-permute-start.7 = (f32[32,1,128]{2,1,0:T(1,128)S(1)}, f32[32,1,128]{2,1,0:T(1,128)S(1)}, u32[]{:S(2)}, u32[]{:S(2)}) collective-permute-start(f32[32,1,128]{2,1,0:T(1,128)S(1)} %copy-done.15), channel_id=1, source_target_pairs={{1,0},{2,1},{3,2},{4,3},{5,4},{6,5},{7,6},{9,8},{10,9},{11,10},{12... | collective-permute-start | bytes 49160 | tf_op jit(solution)/shard_map/ppermute | solution.py:409
  82.5 2.4 %copy-start.3 = (f32[32,128]{1,0:T(8,128)}, f32[32,128]{1,0:T(8,128)S(1)}, u32[]{:S(2)}) copy-start(f32[32,128]{1,0:T(8,128)S(1)} %collective-permute-done.4.before) | copy-start | bytes 49156
  82.6 2.4 %copy-start.4 = (f32[32,128]{1,0:T(8,128)}, f32[32,128]{1,0:T(8,128)S(1)}, u32[]{:S(2)}) copy-start(f32[32,128]{1,0:T(8,128)S(1)} %collective-permute-done.5.after) | copy-start | bytes 49156
  82.6 2.4 %copy-start.5 = (f32[32,1,128]{2,1,0:T(1,128)}, f32[32,1,128]{2,1,0:T(1,128)S(1)}, u32[]{:S(2)}) copy-start(f32[32,1,128]{2,1,0:T(1,128)S(1)} %collective-permute-done.6.lat_before) | copy-start | bytes 49156
  85.0 0.6 copy-start.6
  85.0 0.7 copy-start.2
  95.5 17.1 %collective-permute-start.10 = (f32[32,1,128]{2,1,0:T(1,128)}, f32[32,1,128]{2,1,0:T(1,128)S(1)}, u32[]{:S(2)}, u32[]{:S(2)}) collective-permute-start(f32[32,1,128]{2,1,0:T(1,128)} %get-tuple-element.47), channel_id=1, source_target_pairs={{0,1},{1,2},{2,3},{3,4},{4,5},{5,6},{6,7},{8,9},{9,10},{10,11},{11... | collective-permute-start | bytes 49160 | tf_op jit(solution)/shard_map/ppermute | solution.py:408
  99.1 13.6 %collective-permute-start.11 = (f32[32,1,128]{2,1,0:T(1,128)}, f32[32,1,128]{2,1,0:T(1,128)S(1)}, u32[]{:S(2)}, u32[]{:S(2)}) collective-permute-start(f32[32,1,128]{2,1,0:T(1,128)} %get-tuple-element.48), channel_id=1, source_target_pairs={{1,0},{2,1},{3,2},{4,3},{5,4},{6,5},{7,6},{9,8},{10,9},{11,10},{12... | collective-permute-start | bytes 49160 | tf_op jit(solution)/shard_map/ppermute | solution.py:409
  100.4 12.3 %collective-permute-start.8 = (f32[32,128]{1,0:T(8,128)}, f32[32,128]{1,0:T(8,128)S(1)}, u32[]{:S(2)}, u32[]{:S(2)}) collective-permute-start(f32[32,128]{1,0:T(8,128)} %get-tuple-element.45), channel_id=1, source_target_pairs={{0,8},{8,16},{16,24},{24,0},{1,9},{9,17},{17,25},{25,1},{2,10},{10... | collective-permute-start | bytes 49160 | tf_op jit(solution)/shard_map/ppermute | solution.py:406
  102.6 10.1 %collective-permute-start.9 = (f32[32,128]{1,0:T(8,128)}, f32[32,128]{1,0:T(8,128)S(1)}, u32[]{:S(2)}, u32[]{:S(2)}) collective-permute-start(f32[32,128]{1,0:T(8,128)} %get-tuple-element.46), channel_id=1, source_target_pairs={{8,0},{16,8},{24,16},{0,24},{9,1},{17,9},{25,17},{1,25},{10,2},{18... | collective-permute-start | bytes 49160 | tf_op jit(solution)/shard_map/ppermute | solution.py:407
  112.7 0.6 copy-start.7
  112.7 0.6 copy-start.8
  116.3 30.1 %all-to-all-start.2 = ((f32[352,1,128]{2,1,0:T(1,128)}), f32[352,1,128]{2,1,0:T(1,128)S(1)}, u32[]{:S(2)}, u32[]{:S(2)}) async-start(f32[352,1,128]{2,1,0:T(1,128)} %last_smooth.1), calls=%async_computation.2 | async-start | bytes 360448 | tf_op jit(solution)/shard_map/all_to_all | solution.py:392
  146.5 0.7 copy-start.1
  149.9 0.6 copy-start.19
  (2 other events, 1.2 us)
